TPU v7x, 32 devices: a whole 2x2x4 slice. The times are simulated.
32 devices in a mesh: groups: 2 (over x), expert: 8 (over z, y), sub: 2 (over core).
Axes of the slice: x: 2, y: 2, z: 4, core: 2. Of those that a mesh axis runs over, the one named last changes fastest.
Arguments:
- hidden_state: bfloat16 [2048, 2048], P(('groups', 'expert', 'sub')), parts along dimension 0, may hold values from -6 to 6
- norm_gain: float32 [2048], replicated, may hold values from 0.5 to 1.5
- router_weight: bfloat16 [2048, 16], replicated, may hold values from -0.25 to 0.25
- expert_ids: int32 [2048, 6], P(('groups', 'expert', 'sub')), parts along dimension 0, may hold values from 0 to 15, all different within a row; in each aligned block of 64 rows (0 to 63, 64 to 127, ...) at most 32 rows name the same one
- live_counts: int32 [32], P(('groups', 'expert', 'sub')), parts along dimension 0, may hold values from 16 to 64
- routed_gate_up: bfloat16 [16, 2048, 2816], P(('expert', 'sub')), may hold values from -0.125 to 0.125
- routed_down: bfloat16 [16, 1408, 2048], P(('expert', 'sub')), may hold values from -0.15625 to 0.15625
- shared_weights: bfloat16 [3, 2048, 2816], P(None, None, 'expert'), may hold values from -0.125 to 0.125
Outputs:
- mixed: bfloat16 [2048, 2048], P(('groups', 'expert', 'sub')), parts along dimension 0
- penalty: float32 [2], P('groups'), parts along dimension 0
There are 2 independent parts, one for each index of `groups`. A program takes and returns all parts, laid end to end along the dimension named above; an argument that names none is the same for every part. Nothing has to cross between parts.
Inputs may be any that keep to these rules, and one draw needn't show every extreme that they name: `expert_ids`: in each row the 6 experts differ; among the 64 rows of one device no expert is named more than 32 times.
All inputs are finite; a program needn't handle non-finite values.
Results may differ from a plain program's by a relative error of at most 0.0065.
Values may be sent and summed in bfloat16 or wider, within the bound.
A program may use at most 128 MiB of HBM per device.

v0:
```python
import jax
import jax.numpy as jnp
from jax import lax
from jax.sharding import PartitionSpec as P

BOTH = ("expert", "sub")


def normalize(states, norm_gain):
    values = states.astype(jnp.float32)
    spread = jnp.mean(values * values, axis=-1, keepdims=True)
    return (values * lax.rsqrt(spread + 1e-06) * norm_gain).astype(jnp.bfloat16)


def on_device(
    hidden_state,
    norm_gain,
    router_weight,
    expert_ids,
    live_counts,
    routed_gate_up,
    routed_down,
    shared_weights,
):
    tok_rows, width = hidden_state.shape
    choose = expert_ids.shape[1]
    local_experts = routed_gate_up.shape[0]
    hidden_units = routed_down.shape[1]
    chips = lax.axis_size("expert")
    subs = lax.axis_size("sub")
    devices = chips * subs
    all_experts = local_experts * devices
    all_tokens = tok_rows * devices
    capacity = (tok_rows * choose * 4 + 3 * all_experts - 1) // (3 * all_experts)
    my_sub = lax.axis_index("sub")
    me = lax.axis_index("expert") * subs + my_sub
    normed = normalize(hidden_state, norm_gain)
    everyone = lax.all_gather(normed, BOTH, axis=0, tiled=True)
    probs = jax.nn.sigmoid(jnp.dot(normed, router_weight, preferred_element_type=jnp.float32))
    live = (jnp.arange(tok_rows, dtype=jnp.int32) < live_counts[0]).astype(jnp.float32)
    columns = jnp.arange(all_experts, dtype=jnp.int32)
    hot = jnp.sum((expert_ids[:, :, None] == columns[None, None, :]).astype(jnp.float32), axis=1)
    picked = hot * probs
    weights = live[:, None] * picked / jnp.sum(picked, axis=-1, keepdims=True)
    live_hot = hot * live[:, None]
    notes = jnp.concatenate([weights, live_hot, probs * live[:, None]], axis=-1)
    notes = lax.all_gather(notes, BOTH, axis=0, tiled=True)
    load = jnp.sum(notes[:, all_experts : 2 * all_experts], axis=0)
    mass = jnp.sum(notes[:, 2 * all_experts :], axis=0)
    penalty = all_experts * jnp.sum(load * mass) / (choose * float(all_tokens) * float(all_tokens))
    owner = jnp.arange(all_tokens, dtype=jnp.int32) // tok_rows
    cells = jnp.arange(devices * capacity, dtype=jnp.int32)
    mixed = None
    for item in range(local_experts):
        column = me * local_experts + item
        chosen = lax.dynamic_slice_in_dim(notes, all_experts + column, 1, axis=1)
        weight = lax.dynamic_slice_in_dim(notes, column, 1, axis=1).astype(jnp.bfloat16)
        by_owner = chosen.reshape(devices, tok_rows)
        before = jnp.arange(tok_rows)[:, None] < jnp.arange(tok_rows)[None, :]
        rank = jnp.dot(by_owner, before.astype(jnp.float32)).reshape(all_tokens)
        place = jnp.where(chosen[:, 0] > 0, rank.astype(jnp.int32) + owner * capacity, -1)
        match = place[:, None] == cells[None, :]
        table = match.astype(jnp.bfloat16)
        rows = lax.dot_general(
            table, everyone, (((0,), (0,)), ((), ())), preferred_element_type=jnp.float32
        ).astype(jnp.bfloat16)
        inner = jnp.dot(rows, routed_gate_up[item], preferred_element_type=jnp.float32)
        active = (jax.nn.silu(inner[:, :hidden_units]) * inner[:, hidden_units:]).astype(
            jnp.bfloat16
        )
        results = jnp.dot(active, routed_down[item], preferred_element_type=jnp.float32).astype(
            jnp.bfloat16
        )
        mixing = jnp.where(match, weight, jnp.zeros((), jnp.bfloat16))
        part = jnp.dot(mixing, results, preferred_element_type=jnp.float32)
        mixed = part if mixed is None else mixed + part
    piece = lax.dynamic_index_in_dim(
        everyone.reshape(chips, subs, tok_rows, width), my_sub, axis=1, keepdims=False
    ).reshape(chips * tok_rows, width)
    gate_part = jnp.dot(piece, shared_weights[0], preferred_element_type=jnp.float32)
    up_part = jnp.dot(piece, shared_weights[1], preferred_element_type=jnp.float32)
    shared_active = (jax.nn.silu(gate_part) * up_part).astype(jnp.bfloat16)
    partials = lax.dot_general(
        shared_active,
        shared_weights[2],
        (((1,), (1,)), ((), ())),
        preferred_element_type=jnp.float32,
    )
    mine = (jnp.arange(subs) == my_sub)[None, :, None, None]
    partials = jnp.where(mine, partials.reshape(chips, 1, tok_rows, width), 0.0)
    total = (mixed.reshape(chips, subs, tok_rows, width) + partials).astype(jnp.bfloat16)
    total = total.reshape(all_tokens, width)
    mixed = lax.psum_scatter(total, BOTH, scatter_dimension=0, tiled=True)
    return (mixed.astype(jnp.bfloat16), penalty.reshape(1))


def solution(mesh):
    placed = (
        P(("groups", "expert", "sub"), None),
        P(),
        P(),
        P(("groups", "expert", "sub"), None),
        P(("groups", "expert", "sub")),
        P(("expert", "sub"), None, None),
        P(("expert", "sub"), None, None),
        P(None, None, "expert"),
    )
    return jax.shard_map(
        on_device,
        mesh=mesh,
        in_specs=placed,
        out_specs=(P(("groups", "expert", "sub"), None), P("groups")),
        check_vma=False,
    )
```

profile of v0, /device:TPU:0, one launch (start us, length us, event | category | flops | bytes accessed | tf_op | source)
XLA Modules:
  0.0 185.2 jit_solution(10021006158538988017)
XLA Ops:
  7.2 0.0 copy-start
  7.2 0.0 all-gather.3.cloned.1.call-start
  7.2 1.1 fusion.34
  8.3 1.8 fusion.36
  10.1 0.0 all-gather.3.cloned.1.call-update
  10.2 0.0 reduce-scatter.2.cloned.1.call-start
  10.9 0.7 convert_reduce_fusion
  11.6 0.0 copy-done
  11.6 1.2 multiply_reduce_fusion
  12.8 25.2 %all-gather = f32[16,64,48]{1,2,0:T(8,128)S(1)} all-gather(f32[1,64,48]{1,2,0:T(8,128)S(1)} %maximum_bitcast_fusion), channel_id=1, replica_groups=mesh['groups'=2,'expert'=8,'sub'=2] {'expert','sub'}, dimensions={0}, use_global_device_ids=true | all-gather | bytes 208896 | tf_op jit(solution)/shard_map/all_gather | solution.py:47
  38.0 0.1 copy.18
  38.1 0.2 reshape.107
  38.3 0.1 reshape.101
  38.4 0.1 convolution_convert_fusion.1
  38.5 0.1 convert_element_type.55
  38.6 0.1 broadcast_in_dim.58
  38.7 0.1 broadcast_in_dim.59
  38.8 26.0 %all-gather.3.cloned.1.call-done = bf16[1024,2048]{1,0:T(8,128)(2,1)} async-done(((bf16[64,2048]{1,0:T(8,128)(2,1)}), bf16[1024,2048]{1,0:T(8,128)(2,1)}) %all-gather.3.cloned.1.call-update) | async-done | bytes 4194320 | tf_op jit(solution)/shard_map/all_gather | solution.py:38
  64.8 1.7 constant_dynamic-slice_fusion
  66.5 2.3 %fusion.16 = f32[512,352]{0,1:T(8,128)S(1)} fusion(bf16[512,2048]{1,0:T(8,128)(2,1)S(1)} %bitcast.47, bf16[3,2048,352]{1,2,0:T(8,128)(2,1)} %param.15), kind=kOutput, calls=%fused_computation.17 | convolution fusion | flops 738197504 | bytes 4259840 | tf_op jit(solution)/shard_map/dot_general | solution.py:80
  68.9 2.4 %fusion.25 = bf16[512,352]{0,1:T(8,128)(2,1)S(1)} fusion(bf16[512,2048]{1,0:T(8,128)(2,1)S(1)} %bitcast.48, bf16[3,2048,352]{1,2,0:T(8,128)(2,1)} %param.15, f32[512,352]{0,1:T(8,128)S(1)} %fusion.16), kind=kOutput, calls=%fused_computation.24 | convolution fusion | flops 739278848 | bytes 4620288 | tf_op jit(solution)/shard_map/dot_general | solution.py:81
  71.2 0.2 copy.19
  71.5 4.6 %fusion.12 = f32[8,64,2048]{2,1,0:T(8,128)} fusion(bf16[8,64,352]{2,1,0:T(8,128)(2,1)S(1)} %bitcast.49, bf16[3,2048,352]{1,2,0:T(8,128)(2,1)} %param.15), kind=kOutput, calls=%fused_computation.13 | convolution fusion | flops 738197504 | bytes 5996544 | tf_op jit(solution)/shard_map/dot_general | solution.py:83
  76.1 17.0 %fusion = f32[512,2816]{1,0:T(8,128)} fusion(bf16[1,2048,2816]{2,1,0:T(8,128)(2,1)} %param.13, bf16[1024,2048]{1,0:T(8,128)(2,1)} %all-gather.3.cloned.1.call-done, s32[1024]{0:T(1024)S(1)} %bitcast.51), kind=kOutput, calls=%fused_computation | convolution fusion | flops 8054636544 | bytes 21499904 | tf_op jit(solution)/shard_map/dot_general | solution.py:67
  93.1 0.0 copy-start.1
  93.1 8.1 %fusion.6 = bf16[512,2048]{1,0:T(8,128)(2,1)S(1)} fusion(bf16[1,1408,2048]{2,1,0:T(8,128)(2,1)} %param.14, f32[512,2816]{1,0:T(8,128)} %fusion), kind=kOutput, calls=%fused_computation.8 | convolution fusion | flops 2958163968 | bytes 13631488 | tf_op jit(solution)/shard_map/dot_general | solution.py:71
  101.2 0.0 copy-done.1
  101.2 4.5 %fusion.3 = bf16[1024,2048]{1,0:T(8,128)(2,1)} fusion(f32[8,64,2048]{2,1,0:T(8,128)S(1)} %copy-done.1, pred[1024]{0:T(1024)(128)(4,1)S(1)} %broadcast_in_dim.59, bf16[512,2048]{1,0:T(8,128)(2,1)S(1)} %fusion.6, s32[1024]{0:T(1024)S(1)} %bitcast.52, bf16[1024]{0:T(1024)(128)(2,1)S(1)} %convert_reduce_fusion.1), kind=kOutput, calls=%fused_computation.4 | convolution fusion | flops 2154823680 | bytes 10492928 | tf_op jit(solution)/shard_map/dot_general | solution.py:75
  105.7 0.0 reduce-scatter.2.cloned.1.call-update
  105.7 0.1 slice_reduce_fusion
  105.8 0.6 multiply_reduce_fusion.1
  107.1 70.1 %reduce-scatter.2.cloned.1.call-done = bf16[64,2048]{1,0:T(8,128)(2,1)} async-done(((bf16[1024,2048]{1,0:T(8,128)(2,1)}), bf16[64,2048]{1,0:T(8,128)(2,1)}) %reduce-scatter.2.cloned.1.call-update) | async-done | bytes 262160 | tf_op jit(solution)/shard_map/reduce_scatter | solution.py:93
  (8 shorter events, 0.1 us)
Async XLA Ops:
  7.2 4.4 %copy-start = (bf16[2048,16]{0,1:T(8,128)(2,1)S(1)}, bf16[2048,16]{0,1:T(8,128)(2,1)}, u32[]{:S(2)}) copy-start(bf16[2048,16]{0,1:T(8,128)(2,1)} %param.10) | copy-start | bytes 196612
  7.2 57.6 %all-gather.3.cloned.1.call-start = ((), (), s32[]{:S(2)}) async-start(), calls=%async_computation.1 | async-start | bytes 4456448 | tf_op jit(solution)/shard_map/all_gather | solution.py:38
  10.2 167.0 %reduce-scatter.2.cloned.1.call-start = ((), (), s32[]{:S(2)}) async-start(), calls=%async_computation.2 | async-start | bytes 4456448 | tf_op jit(solution)/shard_map/reduce_scatter | solution.py:93
  93.1 8.1 %copy-start.1 = (f32[8,64,2048]{2,1,0:T(8,128)S(1)}, f32[8,64,2048]{2,1,0:T(8,128)}, u32[]{:S(2)}) copy-start(f32[8,64,2048]{2,1,0:T(8,128)} %fusion.12) | copy-start | bytes 12582916
Sparse Core Ops, SparseCore 0:
  10.7 54.0 all-gather.2
  105.8 71.3 reduce-scatter.1
where the time goes:
time: 186 us; the launch traced here: 185 us
  waiting for transfers between devices  96.1 us (52%)
  matrix products  40.2 us (22%)
  blocking collectives  25.2 us (14%)
  between operations  16.6 us (9%)
  other arithmetic  4.37 us (2%)
  local copies, waits for them, and re-layouts  2.62 us (1%)
    reduce_scatter x1, waiting for transfers between devices, on_device(): mixed = lax.psum_scatter(total, BOTH, scatter_dimension=0, tiled=True)  70.1 us
    all_gather x1, waiting for transfers between devices, on_device(): everyone = lax.all_gather(normed, BOTH, axis=0, tiled=True)  26 us
    all_gather x1, blocking collectives, on_device(): notes = lax.all_gather(notes, BOTH, axis=0, tiled=True)  25.2 us
    dot_general x1, matrix products, on_device(): jnp.dot(rows, routed_gate_up[item], preferred_element_type=jnp.float32)  17 us
    dot_general x1, matrix products, on_device(): jnp.dot(active, routed_down[item], preferred_element_type=jnp.float32)  8.11 us
    dot_general x1, matrix products, on_device(): lax.dot_general(shared_active, shared_weights[2], (((1,), (1,)), ((), ())...  4.65 us
    dot_general x1, matrix products, on_device(): part = jnp.dot(mixing, results, preferred_element_type=jnp.float32)  4.48 us
  transfers between devices with their start and end apart: 2, of which 2 were waited for; matrix products, arithmetic and copies ran while one was open for 2% of the time, Pallas kernels for 0%

commit v1 on v0

--- a/solution.py
+++ b/solution.py
@@ -35,7 +35,6 @@
     my_sub = lax.axis_index("sub")
     me = lax.axis_index("expert") * subs + my_sub
     normed = normalize(hidden_state, norm_gain)
-    everyone = lax.all_gather(normed, BOTH, axis=0, tiled=True)
     probs = jax.nn.sigmoid(jnp.dot(normed, router_weight, preferred_element_type=jnp.float32))
     live = (jnp.arange(tok_rows, dtype=jnp.int32) < live_counts[0]).astype(jnp.float32)
     columns = jnp.arange(all_experts, dtype=jnp.int32)
@@ -44,7 +43,11 @@
     weights = live[:, None] * picked / jnp.sum(picked, axis=-1, keepdims=True)
     live_hot = hot * live[:, None]
     notes = jnp.concatenate([weights, live_hot, probs * live[:, None]], axis=-1)
-    notes = lax.all_gather(notes, BOTH, axis=0, tiled=True)
+    everyone, notes = jnp.split(
+        lax.all_gather(jnp.concatenate([normed, notes], axis=1), BOTH, axis=0, tiled=True),
+        [normed.shape[1]],
+        axis=1,
+    )
     load = jnp.sum(notes[:, all_experts : 2 * all_experts], axis=0)
     mass = jnp.sum(notes[:, 2 * all_experts :], axis=0)
     penalty = all_experts * jnp.sum(load * mass) / (choose * float(all_tokens) * float(all_tokens))

time: 186 us -> 219 us (1.18)
  waiting for transfers between devices: 96.1 us -> 149 us
  blocking collectives: 25.2 us -> 0 us
  local copies, waits for them, and re-layouts: 2.62 us -> 8.39 us
    all_gather x1, waiting for transfers between devices: 26 us -> 80.2 us  [on_device(): lax.all_gather(jnp.concatenate([normed, notes], axis=1), BOTH, axis=0, ti...]
    all_gather x1 -> x0, blocking collectives: 25.2 us -> none  [on_device(): notes = lax.all_gather(notes, BOTH, axis=0, tiled=True)]
    split x0 -> x2, local copies, waits for them, and re-layouts: none -> 5.29 us  [on_device(): jnp.split(lax.all_gather(jnp.concatenate([normed, notes], axis=1), BOTH,...]
  transfers between devices with their start and end apart: 2 -> 2, of which waited for: 2 -> 2; matrix products, arithmetic and copies ran while one was open for 2% -> 1% of each run, Pallas kernels for 0% -> 0%
where the time goes in v1:
time: 219 us; the launch traced here: 218 us
  waiting for transfers between devices  149 us (68%)
  matrix products  38.7 us (18%)
  between operations  16.6 us (8%)
  local copies, waits for them, and re-layouts  8.39 us (4%)
  other arithmetic  5.52 us (3%)
    all_gather x1, waiting for transfers between devices, on_device(): lax.all_gather(jnp.concatenate([normed, notes], axis=1), BOTH, axis=0, ti...  80.2 us
    reduce_scatter x1, waiting for transfers between devices, on_device(): mixed = lax.psum_scatter(total, BOTH, scatter_dimension=0, tiled=True)  68.6 us
    dot_general x1, matrix products, on_device(): jnp.dot(rows, routed_gate_up[item], preferred_element_type=jnp.float32)  18.3 us
    dot_general x1, matrix products, on_device(): jnp.dot(active, routed_down[item], preferred_element_type=jnp.float32)  7.95 us
    split x2, local copies, waits for them, and re-layouts, on_device(): jnp.split(lax.all_gather(jnp.concatenate([normed, notes], axis=1), BOTH,...  5.29 us
    dot_general x1, matrix products, on_device(): lax.dot_general(shared_active, shared_weights[2], (((1,), (1,)), ((), ())...  4.61 us
    dot_general x1, matrix products, on_device(): part = jnp.dot(mixing, results, preferred_element_type=jnp.float32)  4.54 us
  transfers between devices with their start and end apart: 2, of which 2 were waited for; matrix products, arithmetic and copies ran while one was open for 1% of the time, Pallas kernels for 0%

profile of v1, /device:TPU:0, one launch (start us, length us, event | category | flops | bytes accessed | tf_op | source)
XLA Modules:
  0.0 218.2 jit_solution(11808483793336607937)
XLA Ops:
  7.2 0.0 copy-start
  7.2 0.0 all-gather.2.cloned.1.call-start
  7.9 1.1 fusion.34
  9.0 0.7 convert_reduce_fusion
  9.7 1.1 fusion.48
  10.8 0.0 copy-done
  10.8 1.2 multiply_reduce_fusion
  12.1 0.1 copy.24
  12.1 0.1 copy.22
  12.2 0.1 copy.23
  12.3 1.0 concatenate.3
  13.3 0.0 all-gather.2.cloned.1.call-update
  13.3 0.0 reduce-scatter.2.cloned.1.call-start
  13.4 0.1 broadcast_in_dim.58
  13.4 0.1 broadcast_in_dim.59
  13.5 80.2 %all-gather.2.cloned.1.call-done = f32[1024,2096]{1,0:T(8,128)} async-done(((f32[64,2096]{1,0:T(8,128)}), f32[1024,2096]{1,0:T(8,128)}) %all-gather.2.cloned.1.call-update) | async-done | bytes 8585232 | tf_op jit(solution)/shard_map/all_gather | solution.py:47
  93.8 1.1 split.8
  94.9 0.3 fusion.46
  95.2 0.4 dynamic-slice_reduce_fusion
  95.5 0.1 reshape.101
  95.6 0.1 convolution_convert_fusion.1
  95.8 0.5 convert_element_type.66
  96.2 0.0 slice-start
  96.2 0.4 fusion.40
  96.6 0.0 slice-start.1
  96.6 4.2 %split.9 = bf16[1024,2048]{1,0:T(8,128)(2,1)S(1)} slice(f32[1024,2096]{1,0:T(8,128)} %all-gather.2.cloned.1.call-done), slice={[0:1024], [0:2048]} | slice | bytes 8388608 | tf_op jit(solution)/shard_map/split | solution.py:46
  100.9 0.2 constant_dynamic-slice_fusion
  101.1 0.0 slice-done
  101.1 0.0 slice-done.1
  101.1 0.9 fusion.16
  102.1 1.0 fusion.25
  103.1 0.2 copy.26
  103.3 4.6 %fusion.12 = f32[8,64,2048]{2,1,0:T(8,128)} fusion(bf16[8,64,352]{2,1,0:T(8,128)(2,1)S(1)} %bitcast.43, bf16[3,2048,352]{1,2,0:T(8,128)(2,1)} %param.15), kind=kOutput, calls=%fused_computation.13 | convolution fusion | flops 738197504 | bytes 5996544 | tf_op jit(solution)/shard_map/dot_general | solution.py:86
  107.9 18.3 %fusion = f32[512,2816]{1,0:T(8,128)} fusion(bf16[1,2048,2816]{2,1,0:T(8,128)(2,1)} %param.13, s32[1024]{0:T(1024)S(1)} %fusion.40, f32[1024,2096]{1,0:T(8,128)} %all-gather.2.cloned.1.call-done), kind=kOutput, calls=%fused_computation | convolution fusion | flops 8053587968 | bytes 21499904 | tf_op jit(solution)/shard_map/dot_general | solution.py:70
  126.2 0.0 copy-start.1
  126.2 7.9 %fusion.6 = bf16[512,2048]{1,0:T(8,128)(2,1)S(1)} fusion(bf16[1,1408,2048]{2,1,0:T(8,128)(2,1)} %param.14, f32[512,2816]{1,0:T(8,128)} %fusion), kind=kOutput, calls=%fused_computation.8 | convolution fusion | flops 2958163968 | bytes 13631488 | tf_op jit(solution)/shard_map/dot_general | solution.py:74
  134.2 0.0 copy-done.1
  134.2 4.5 %fusion.3 = bf16[1024,2048]{1,0:T(8,128)(2,1)} fusion(f32[8,64,2048]{2,1,0:T(8,128)S(1)} %copy-done.1, pred[1024]{0:T(1024)(128)(4,1)S(1)} %broadcast_in_dim.59, bf16[512,2048]{1,0:T(8,128)(2,1)S(1)} %fusion.6, s32[1024]{0:T(1024)S(1)} %fusion.40, bf16[1024]{0:T(1024)(128)(2,1)S(1)} %fusion.46), kind=kOutput, calls=%fused_computation.4 | convolution fusion | flops 2154823680 | bytes 10492928 | tf_op jit(solution)/shard_map/dot_general | solution.py:78
  138.7 0.0 reduce-scatter.2.cloned.1.call-update
  138.8 1.6 slice_reduce_fusion
  140.4 0.6 multiply_reduce_fusion.1
  141.6 68.6 %reduce-scatter.2.cloned.1.call-done = bf16[64,2048]{1,0:T(8,128)(2,1)} async-done(((bf16[1024,2048]{1,0:T(8,128)(2,1)}), bf16[64,2048]{1,0:T(8,128)(2,1)}) %reduce-scatter.2.cloned.1.call-update) | async-done | bytes 262160 | tf_op jit(solution)/shard_map/reduce_scatter | solution.py:96
  (5 shorter events, 0.0 us)
Async XLA Ops:
  7.2 3.6 %copy-start = (bf16[2048,16]{0,1:T(8,128)(2,1)S(1)}, bf16[2048,16]{0,1:T(8,128)(2,1)}, u32[]{:S(2)}) copy-start(bf16[2048,16]{0,1:T(8,128)(2,1)} %param.10) | copy-start | bytes 196612
  7.2 86.6 %all-gather.2.cloned.1.call-start = ((), (), s32[]{:S(2)}) async-start(), calls=%async_computation.1 | async-start | bytes 9469952 | tf_op jit(solution)/shard_map/all_gather | solution.py:47
  13.3 197.0 %reduce-scatter.2.cloned.1.call-start = ((), (), s32[]{:S(2)}) async-start(), calls=%async_computation.2 | async-start | bytes 4456448 | tf_op jit(solution)/shard_map/reduce_scatter | solution.py:96
  96.2 4.9 %slice-start = ((s8[4325376]{0:T(1024)(128)(4,1)}), s8[4194304]{0:T(1024)(128)(4,1)S(1)}, s32[]{:S(2)}) async-start(s8[4325376]{0:T(1024)(128)(4,1)} %bitcast.44), calls=%async_computation.3 | async-start | bytes 8388608
  96.6 4.5 %slice-start.1 = ((s8[4325376]{0:T(1024)(128)(4,1)}), s8[131072]{0:T(1024)(128)(4,1)S(1)}, s32[]{:S(2)}) async-start(s8[4325376]{0:T(1024)(128)(4,1)} %bitcast.44), calls=%async_computation.4 | async-start | bytes 262144
  126.2 8.0 %copy-start.1 = (f32[8,64,2048]{2,1,0:T(8,128)S(1)}, f32[8,64,2048]{2,1,0:T(8,128)}, u32[]{:S(2)}) copy-start(f32[8,64,2048]{2,1,0:T(8,128)} %fusion.12) | copy-start | bytes 12582916
Sparse Core Ops, SparseCore 0:
  13.4 80.3 all-gather.1
  138.9 71.3 reduce-scatter.1
